TPU v7x, 128 devices: a whole 4x4x4 slice. The times are simulated.
128 devices in a mesh: data: 128 (over z, y, x, core).
Axes of the slice: x: 4, y: 4, z: 4, core: 2. Of those that a mesh axis runs over, the one named last changes fastest.
Arguments:
- tokens: bfloat16 [262144, 1024], P('data')
- w_up: bfloat16 [1024, 4096], replicated
- w_down: bfloat16 [4096, 1024], replicated
- heads: bfloat16 [4, 1024, 3], replicated
- labels: int32 [4, 262144], P(None, 'data')
Outputs:
- output 1: float32 [4], replicated
- output 2: float32 [1024, 4096], P('data')
- output 3: float32 [4096, 1024], P('data')
All inputs are finite; a program needn't handle non-finite values.
Results may differ from a plain program's by a relative error of at most 0.001.
Values are sent between devices in bfloat16 or wider.
A program may use at most 1 GiB of HBM per device.

v0:
```python
import jax
import jax.numpy as jnp
from jax import lax
from jax.sharding import PartitionSpec as P

SOLVER_STEPS = 20
EXACT_PREC = lax.Precision.HIGHEST


def solve_weights(full_gram):
    num_tasks = full_gram.shape[0]
    step_scale = jnp.trace(full_gram) / num_tasks

    def update(step_idx, mix_wts):
        descent = jnp.sum(full_gram * mix_wts[None, :], axis=1)
        mix_wts = mix_wts * jnp.exp(-descent / step_scale)
        return mix_wts / jnp.sum(mix_wts)

    uniform_start = jnp.full((num_tasks,), 1.0 / num_tasks, jnp.float32)
    return lax.fori_loop(0, SOLVER_STEPS, update, uniform_start)


def solution(mesh):
    group_size = mesh.shape['data']

    def local_step(tok_rows, w_up, w_down, heads, label_rows):
        total_rows = tok_rows.shape[0] * group_size
        num_classes = heads.shape[2]
        pre_act = jnp.dot(tok_rows, w_up, preferred_element_type=jnp.float32).astype(jnp.bfloat16)
        hidden = jax.nn.gelu(pre_act.astype(jnp.float32)).astype(jnp.bfloat16)
        trunk_out = tok_rows.astype(jnp.float32) + jnp.dot(hidden, w_down, preferred_element_type=jnp.float32)
        logits = jnp.einsum('bd,tdc->tbc', trunk_out.astype(jnp.bfloat16), heads, preferred_element_type=jnp.float32)
        onehot = (label_rows[:, :, None] == jnp.arange(num_classes)[None, None, :]).astype(jnp.float32)
        task_resid = (jax.nn.softmax(logits, axis=-1) - onehot) / total_rows
        heads_f32 = heads.astype(jnp.float32)
        head_gram = jnp.einsum('tdc,sde->tcse', heads_f32, heads_f32, precision=EXACT_PREC)
        res_outer = jnp.einsum('tbc,sbe->tcse', task_resid, task_resid, precision=EXACT_PREC)
        part_gram = jnp.sum(res_outer * head_gram, axis=(1, 3))
        full_gram = lax.psum(part_gram, 'data')
        mix_wts = solve_weights(full_gram)
        d_out = jnp.einsum('tbc,tdc->bd', task_resid * mix_wts[:, None, None], heads_f32, precision=EXACT_PREC).astype(jnp.bfloat16)
        grad_down = lax.dot_general(hidden, d_out, (((0,), (0,)), ((), ())), preferred_element_type=jnp.float32)
        d_hidden = lax.dot_general(d_out, w_down, (((1,), (1,)), ((), ())), preferred_element_type=jnp.float32)
        gelu_vjp = jax.vjp(jax.nn.gelu, pre_act.astype(jnp.float32))[1]
        d_pre = gelu_vjp(d_hidden)[0].astype(jnp.bfloat16)
        grad_up = lax.dot_general(tok_rows, d_pre, (((0,), (0,)), ((), ())), preferred_element_type=jnp.float32)
        up_shard = lax.psum_scatter(grad_up, 'data', scatter_dimension=0, tiled=True)
        down_shard = lax.psum_scatter(grad_down, 'data', scatter_dimension=0, tiled=True)
        return mix_wts, up_shard, down_shard

    return jax.shard_map(local_step, mesh=mesh, in_specs=(P('data', None), P(), P(), P(), P(None, 'data')), out_specs=(P(), P('data', None), P('data', None)), check_vma=False)
```

profile of v0, /device:TPU:0, one launch (start us, length us, event | category | flops | bytes accessed | tf_op | source)
XLA Modules:
  0.0 1593.8 jit_solution(17166409505334736600)
XLA Ops:
  7.2 24.2 %convolution_convert_fusion = bf16[2048,4096]{1,0:T(8,128)(2,1)} fusion(bf16[2048,1024]{1,0:T(8,128)(2,1)} %param.7, bf16[1024,4096]{1,0:T(8,128)(2,1)} %param.8), kind=kOutput, calls=%fused_computation.20 | convolution fusion | flops 17188257792 | bytes 29360128 | tf_op jit(solution)/shard_map/dot_general | solution.py:29
  31.4 28.5 %fusion.48 = (f32[4,2048]{1,0:T(4,128)S(1)}, f32[4,2048,3]{1,0,2:T(4,128)S(1)}) fusion(bf16[4,1024,3]{1,0,2:T(4,128)(2,1)S(1)} %copy-done, bf16[4096,1024]{1,0:T(8,128)(2,1)} %param.9, bf16[2048,4096]{1,0:T(8,128)(2,1)} %convolution_convert_fusion, bf16[2048,1024]{1,0:T(8,128)(2,1)} %param.7), kind=kOutput, calls=%fused_computation.55 | convolution fusion | flops 17320394752 | bytes 29515776 | tf_op jit(solution)/shard_map/bd,tdc->tbc/dot_general | solution.py:32
  60.0 1.3 fusion.23
  61.6 68.5 %psum.7 = f32[4,4]{1,0:T(4,128)S(1)} all-reduce(f32[4,4]{1,0:T(4,128)S(1)} %fusion.22), channel_id=1, replica_groups=mesh['data'=128] {'data'}, use_global_device_ids=true, to_apply=%region_3.0 | all-reduce | flops 16 | bytes 128 | tf_op jit(solution)/shard_map/psum | solution.py:39
  131.3 28.4 %while.11 = (s32[]{:T(128)}, f32[4]{0:T(128)S(1)}, f32[4,4]{1,0:T(4,128)S(1)}, f32[]{:T(128)}, s32[]{:T(128)}, /*index=5*/s32[]{:T(128)}) while((s32[]{:T(128)}, f32[4]{0:T(128)S(1)}, f32[4,4]{1,0:T(4,128)S(1)}, f32[]{:T(128)}, s32[]{:T(128)}, /*index=5*/s32[]{:T(128)}) %tuple.32), condition=%wide.region_8.9_spmd.clone, body=%wide.region_5.8_spmd.clone.sunk | while | flops 58 | bytes 300 | solution.py:20
  132.0 0.6 broadcast_divide_fusion.2
  133.5 0.6 broadcast_divide_fusion.2
  134.9 0.6 broadcast_divide_fusion.2
  136.3 0.6 broadcast_divide_fusion.2
  137.7 0.6 broadcast_divide_fusion.2
  139.1 0.6 broadcast_divide_fusion.2
  140.6 0.6 broadcast_divide_fusion.2
  142.0 0.6 broadcast_divide_fusion.2
  143.4 0.6 broadcast_divide_fusion.2
  144.8 0.6 broadcast_divide_fusion.2
  146.2 0.6 broadcast_divide_fusion.2
  147.7 0.6 broadcast_divide_fusion.2
  149.1 0.6 broadcast_divide_fusion.2
  150.5 0.6 broadcast_divide_fusion.2
  151.9 0.6 broadcast_divide_fusion.2
  153.3 0.6 broadcast_divide_fusion.2
  154.8 0.6 broadcast_divide_fusion.2
  156.2 0.6 broadcast_divide_fusion.2
  157.6 0.6 broadcast_divide_fusion.2
  159.0 0.6 broadcast_divide_fusion.2
  159.7 3.9 bitcast_convert_fusion
  163.6 44.7 %fusion.69 = bf16[2048,4096]{1,0:T(8,128)(2,1)} fusion(bf16[2048,4096]{1,0:T(8,128)(2,1)} %convolution_convert_fusion, bf16[2048,1024]{1,0:T(8,128)(2,1)S(1)} %bitcast_convert_fusion, bf16[4096,1024]{1,0:T(8,128)(2,1)} %param.9), kind=kOutput, calls=%fused_computation.12.clone.clone.clone.clone.1 | convolution fusion | flops 17356029952 | bytes 46137344 | tf_op jit(solution)/shard_map/dot_general | solution.py:43
  208.3 23.0 %fusion.12 = f32[1024,4096]{0,1:T(8,128)} fusion(bf16[2048,1024]{1,0:T(8,128)(2,1)S(1)} %copy-done.4, bf16[2048,4096]{1,0:T(8,128)(2,1)} %fusion.69), kind=kOutput, calls=%fused_computation.21 | convolution fusion | flops 17179869184 | bytes 37748736 | tf_op jit(solution)/shard_map/dot_general | solution.py:46
  231.4 17.5 %copy.12 = f32[1024,4096]{1,0:T(8,128)} copy(f32[1024,4096]{0,1:T(8,128)} %fusion.12) | data formatting | bytes 33554432
  248.9 28.9 %fusion.40 = f32[4096,1024]{1,0:T(8,128)} fusion(bf16[2048,1024]{1,0:T(8,128)(2,1)} %copy-done.5, bf16[2048,4096]{1,0:T(8,128)(2,1)} %convolution_convert_fusion), kind=kOutput, calls=%fused_computation.53 | convolution fusion | flops 17263755264 | bytes 37748736 | tf_op jit(solution)/shard_map/dot_general | solution.py:42
  277.8 639.8 %reduce-scatter.7.cloned.1.call-done = f32[8,4096]{1,0:T(8,128)} async-done(((f32[1024,4096]{1,0:T(8,128)}), f32[8,4096]{1,0:T(8,128)}) %reduce-scatter.7.cloned.1.call-update) | async-done | bytes 131088
  917.7 668.8 %reduce-scatter.5.cloned.1.call-done = f32[32,1024]{1,0:T(8,128)} async-done(((f32[4096,1024]{1,0:T(8,128)}), f32[32,1024]{1,0:T(8,128)}) %reduce-scatter.5.cloned.1.call-update) | async-done | bytes 131088 | tf_op jit(solution)/shard_map/reduce_scatter | solution.py:48
  (82 shorter events, 15.9 us)
Async XLA Ops:
  7.2 24.3 %copy-start = (bf16[4,1024,3]{1,0,2:T(4,128)(2,1)S(1)}, bf16[4,1024,3]{1,0,2:T(4,128)(2,1)}, u32[]{:S(2)}) copy-start(bf16[4,1024,3]{1,0,2:T(4,128)(2,1)} %param.10) | copy-start | bytes 73732
  7.2 910.5 %reduce-scatter.7.cloned.1.call-start = ((), (), s32[]{:S(2)}) async-start(), calls=%async_computation.3 | async-start | bytes 16908288
  31.4 28.5 %copy-start.2 = (s32[4,2048]{1,0:T(4,128)S(1)}, s32[4,2048]{1,0:T(4,128)}, u32[]{:S(2)}) copy-start(s32[4,2048]{1,0:T(4,128)} %param.11) | copy-start | bytes 98308
  159.7 48.6 %copy-start.3 = (f32[4]{0:T(128)}, f32[4]{0:T(128)S(1)}, u32[]{:S(2)}) copy-start(f32[4]{0:T(128)S(1)} %get-tuple-element.44) | copy-start | bytes 52
  163.6 44.7 %copy-start.5 = (bf16[2048,1024]{1,0:T(8,128)(2,1)}, bf16[2048,1024]{1,0:T(8,128)(2,1)S(1)}, u32[]{:S(2)}) copy-start(bf16[2048,1024]{1,0:T(8,128)(2,1)S(1)} %bitcast_convert_fusion) | copy-start | bytes 12582916
  163.6 44.7 %copy-start.4 = (bf16[2048,1024]{1,0:T(8,128)(2,1)S(1)}, bf16[2048,1024]{1,0:T(8,128)(2,1)}, u32[]{:S(2)}) copy-start(bf16[2048,1024]{1,0:T(8,128)(2,1)} %param.7) | copy-start | bytes 12582916
  248.8 1337.7 %reduce-scatter.5.cloned.1.call-start = ((), (), s32[]{:S(2)}) async-start(), calls=%async_computation.2 | async-start | bytes 16908288 | tf_op jit(solution)/shard_map/reduce_scatter | solution.py:48
  248.9 1337.6 %copy-start.1 = (bf16[4,1024,3]{1,0,2:T(4,128)(2,1)S(1)}, bf16[4,1024,3]{1,0,2:T(4,128)(2,1)}, u32[]{:S(2)}) copy-start(bf16[4,1024,3]{1,0,2:T(4,128)(2,1)} %param.10) | copy-start | bytes 73732
Sparse Core Ops, SparseCore 0:
  249.0 668.6 reduce-scatter.6
  920.6 665.8 reduce-scatter.4
where the time goes:
time: 1600 us; the launch traced here: 1590 us
  waiting for transfers between devices  1310 us (82%)
  matrix products  155 us (10%)
  blocking collectives  68.5 us (4%)
  other arithmetic  28.4 us (2%)
  local copies, waits for them, and re-layouts  17.5 us (1%)
    reduce_scatter x1, waiting for transfers between devices, local_step(): lax.psum_scatter(grad_down, 'data', scatter_dimension=0, tiled=True)  669 us
    unnamed x3, waiting for transfers between devices  640 us
    psum x1, blocking collectives, local_step(): full_gram = lax.psum(part_gram, 'data')  68.5 us
    dot_general x1, matrix products, local_step(): lax.dot_general(d_out, w_down, (((1,), (1,)), ((), ())), preferred_elemen...  44.7 us
  transfers between devices with their start and end apart: 2, of which 2 were waited for; matrix products, arithmetic and copies ran while one was open for 2% of the time, Pallas kernels for 0%

commit v1 on v0

v1 whole, which is shorter than its diff:
```python
import functools

import jax
import jax.numpy as jnp
from jax import lax
from jax.experimental import pallas as pl
from jax.experimental.pallas import tpu as pltpu
from jax.sharding import PartitionSpec as P

SOLVER_STEPS = 20
EXACT_PREC = lax.Precision.HIGHEST
MESH = pl.DeviceIdType.MESH
VMEM_BYTES = 67_043_328
ROWS = 8


def coords(me):
    return me % 2, (me // 2) % 4, (me // 8) % 4, me // 32


def axis_of(k, x, y, z):
    wz = (k - 1) * (k - 2) // 2
    wy = k * (2 - k)
    wx = k * (k - 1) // 2
    return z * wz + y * wy + x * wx, 32 * wz + 8 * wy + 2 * wx


def enter(peers):
    barrier = pltpu.get_barrier_semaphore()
    for peer in peers:
        pl.semaphore_signal(barrier, inc=1, device_id=(peer,), device_id_type=MESH)
    pl.semaphore_wait(barrier, len(peers))


def gram_kernel(gram_ref, wts_ref, stage0, stage1, stage2, tot0, tot1, send_sem, recv_sem):
    me = lax.axis_index('data')
    c, x, y, z = coords(me)
    low = me % 8
    group0 = [me - low + (low + d) % 8 for d in range(1, 8)]
    group1 = [me + ((y + d) % 4 - y) * 8 for d in range(1, 4)]
    group2 = [me + ((z + d) % 4 - z) * 32 for d in range(1, 4)]
    enter(group0 + group1 + group2)

    def exchange(src, slots, slot, group, first):
        copies = []
        for n, peer in enumerate(group):
            copy = pltpu.make_async_remote_copy(
                src_ref=src,
                dst_ref=slots.at[slot],
                send_sem=send_sem.at[first + n],
                recv_sem=recv_sem.at[first + n],
                device_id=(peer,),
                device_id_type=MESH,
            )
            copy.start()
            copies.append(copy)
        slots[slot] = src[...]
        for copy in copies:
            copy.wait()

    exchange(gram_ref, stage0, low, group0, 0)
    tot0[...] = sum(stage0[n] for n in range(1, 8)) + stage0[0]
    exchange(tot0, stage1, y, group1, 7)
    tot1[...] = (stage1[0] + stage1[1]) + (stage1[2] + stage1[3])
    exchange(tot1, stage2, z, group2, 10)
    full = (stage2[0] + stage2[1]) + (stage2[2] + stage2[3])
    gram, gram_t = full[0], full[1]
    row = lax.broadcasted_iota(jnp.int32, gram.shape, 0)
    lane = lax.broadcasted_iota(jnp.int32, gram.shape, 1)
    trace = jnp.sum(jnp.where(row == lane, gram, 0.0), axis=(0, 1), keepdims=True)
    scale = jnp.broadcast_to(trace / 4, gram.shape)
    by_lane = jnp.where(lane < 4, 0.25, 0.0)
    by_row = jnp.where(row < 4, 0.25, 0.0)
    for _ in range(SOLVER_STEPS):
        down_row = jnp.sum(gram * by_lane, axis=1, keepdims=True)
        down_lane = jnp.sum(gram_t * by_row, axis=0, keepdims=True)
        by_row = by_row * jnp.exp(-down_row / scale)
        by_lane = by_lane * jnp.exp(-down_lane / scale)
        by_row = by_row / jnp.sum(by_row, axis=0, keepdims=True)
        by_lane = by_lane / jnp.sum(by_lane, axis=1, keepdims=True)
    wts_ref[...] = by_lane


def solve_weights(part_gram):
    pads = ((0, 0), (0, 4), (0, 124))
    both = jnp.pad(jnp.stack([part_gram, part_gram.T]), pads)
    wts = pl.pallas_call(
        gram_kernel,
        out_shape=jax.ShapeDtypeStruct((8, 128), jnp.float32),
        in_specs=[pl.BlockSpec(memory_space=pltpu.VMEM)],
        out_specs=pl.BlockSpec(memory_space=pltpu.VMEM),
        scratch_shapes=[
            pltpu.VMEM((8, 2, 8, 128), jnp.float32),
            pltpu.VMEM((4, 2, 8, 128), jnp.float32),
            pltpu.VMEM((4, 2, 8, 128), jnp.float32),
            pltpu.VMEM((2, 8, 128), jnp.float32),
            pltpu.VMEM((2, 8, 128), jnp.float32),
            pltpu.SemaphoreType.DMA((13,)),
            pltpu.SemaphoreType.DMA((13,)),
        ],
        compiler_params=pltpu.CompilerParams(collective_id=0, has_side_effects=True),
    )(both)
    return wts[0, :4]


def scatter_kernel(n_down, n_up, width, down_ref, up_ref, out_down, out_up, src, pair_in, work, opp_r, opp_l, from_l, from_r,
                   mid, mid_in, low, low_in, load_sem, pair_s, pair_r, s1, r1, s2, r2, s3, r3):
    count = n_down + n_up
    per_row = down_ref.shape[4] // width
    me = lax.axis_index('data')
    c, x, y, z = coords(me)
    partner = me + 1 - 2 * c
    everyone = [partner]
    for k in range(3):
        pos, stride = axis_of(k, x, y, z)
        everyone += [me + ((pos + d) % 4 - pos) * stride for d in range(1, 4)]
    enter(everyone)

    def axes(u):
        return [axis_of((u + n) % 3, x, y, z) for n in range(3)]

    def remote(a, b, s, r, peer):
        return pltpu.make_async_remote_copy(
            src_ref=a, dst_ref=b, send_sem=s, recv_sem=r, device_id=(peer,), device_id_type=MESH)

    def load_down(u):
        cols = pl.ds(pl.multiple_of((u % per_row) * width, width), width)
        return pltpu.make_async_copy(down_ref.at[:, :, u // per_row, :, cols], src.at[u % 3], load_sem.at[u % 3])

    def load_up(u):
        cols = pl.ds(pl.multiple_of((u - n_down) * width, width), width)
        return pltpu.make_async_copy(up_ref.at[:, :, :, cols], src.at[u % 3], load_sem.at[u % 3])

    def start_load(u):
        @pl.when(u < n_down)
        def _():
            load_down(u).start()

        @pl.when(u >= n_down)
        def _():
            load_up(u).start()

    def pair_copy(u):
        return remote(src.at[u % 3, :, 1 - c], pair_in.at[u], pair_s.at[u], pair_r.at[u], partner)

    def first_copies(u):
        pos, stride = axes(u)[0]
        right = me + ((pos + 1) % 4 - pos) * stride
        left = me + ((pos + 3) % 4 - pos) * stride
        at_r, at_l, at_o = 16 * ((pos + 1) % 4), 16 * ((pos + 3) % 4), 16 * ((pos + 2) % 4)
        buf = work.at[u % 5]
        ends = [
            (at_o, opp_r.at[u], right),
            (at_o + 8, opp_l.at[u], left),
            (at_r + 8, from_l.at[u, pl.ds(8, 8)], right),
            (at_l, from_r.at[u, pl.ds(0, 8)], left),
            (at_r, from_l.at[u, pl.ds(0, 8)], right),
            (at_l + 8, from_r.at[u, pl.ds(8, 8)], left),
        ]
        return [remote(buf.at[pl.ds(at, 8)], dst, s1.at[u, n], r1.at[u, n], peer) for n, (at, dst, peer) in enumerate(ends)]

    def second_copies(u):
        pos, stride = axes(u)[1]
        return [remote(mid.at[u % 3, pl.ds(4 * ((pos + d) % 4), 4)], mid_in.at[u, d - 1], s2.at[u, d - 1], r2.at[u, d - 1],
                       me + ((pos + d) % 4 - pos) * stride) for d in range(1, 4)]

    def third_copies(u):
        pos, stride = axes(u)[2]
        return [remote(low.at[u % 3, (pos + d) % 4], low_in.at[u, d - 1], s3.at[u, d - 1], r3.at[u, d - 1],
                       me + ((pos + d) % 4 - pos) * stride) for d in range(1, 4)]

    def within(u):
        return jnp.logical_and(u >= 0, u < count)

    start_load(0)

    def body(t, _):
        @pl.when(t + 1 < count)
        def _():
            start_load(t + 1)

        @pl.when(t < count)
        def _():
            pltpu.make_async_copy(up_ref.at[:, :, :, pl.ds(0, width)], src.at[t % 3], load_sem.at[t % 3]).wait()
            pair_copy(t).start()

        ub = t - 1

        @pl.when(within(ub))
        def _():
            copy = pair_copy(ub)
            copy.wait_recv()
            (_, st1), (_, st2), (_, st3) = axes(ub)

            def add(b, _):
                at = (b // 4) * (st1 // 2) + (b % 4) * (st2 // 2)
                for n in range(4):
                    here = at + n * (st3 // 2)
                    work[ub % 5, 4 * b + n] = src[ub % 3, here, c] + pair_in[ub, here]
                return 0

            lax.fori_loop(0, 16, add, 0)
            copy.wait_send()
            for copy in first_copies(ub)[:4]:
                copy.start()

        uc = t - 3

        @pl.when(within(uc))
        def _():
            copies = first_copies(uc)
            (pos, _), _, _ = axes(uc)
            at_r, at_l = 16 * ((pos + 1) % 4), 16 * ((pos + 3) % 4)
            copies[0].wait_recv()
            work[uc % 5, pl.ds(at_r, 8)] += opp_r[uc]
            copies[4].start()
            copies[1].wait_recv()
            work[uc % 5, pl.ds(at_l + 8, 8)] += opp_l[uc]
            copies[5].start()

        ud = t - 5

        @pl.when(within(ud))
        def _():
            copies = first_copies(ud)
            for copy in copies[2:]:
                copy.wait_recv()
            (pos, _), _, _ = axes(ud)
            for n in range(0, 16, 4):
                mid[ud % 3, pl.ds(n, 4)] = (work[ud % 5, pl.ds(16 * pos + n, 4)] + from_l[ud, pl.ds(n, 4)]) + from_r[ud, pl.ds(n, 4)]
            for copy in second_copies(ud):
                copy.start()
            for copy in copies:
                copy.wait_send()

        ue = t - 7

        @pl.when(within(ue))
        def _():
            copies = second_copies(ue)
            for copy in copies:
                copy.wait_recv()
            _, (pos, _), _ = axes(ue)
            low[ue % 3] = (mid[ue % 3, pl.ds(4 * pos, 4)] + mid_in[ue, 0]) + (mid_in[ue, 1] + mid_in[ue, 2])
            for copy in third_copies(ue):
                copy.start()
            for copy in copies:
                copy.wait_send()

        uf = t - 9

        @pl.when(within(uf))
        def _():
            copies = third_copies(uf)
            for copy in copies:
                copy.wait_recv()
            _, _, (pos, _) = axes(uf)
            total = (low[uf % 3, pos] + low_in[uf, 0]) + (low_in[uf, 1] + low_in[uf, 2])

            @pl.when(uf < n_down)
            def _():
                out_down[uf // per_row, :, pl.ds(pl.multiple_of((uf % per_row) * width, width), width)] = total

            @pl.when(uf >= n_down)
            def _():
                out_up[:, pl.ds(pl.multiple_of((uf - n_down) * width, width), width)] = total

            for copy in copies:
                copy.wait_send()

        return 0

    lax.fori_loop(0, count + 9, body, 0)


def scatter_grads(grad_down, grad_up, width):
    hidden, model = grad_down.shape
    tiles = hidden // 128 // ROWS
    n_down = tiles * (model // width)
    n_up = hidden // width
    count = n_down + n_up
    f32 = jnp.float32
    block = (ROWS, width)
    out_down, out_up = pl.pallas_call(
        functools.partial(scatter_kernel, n_down, n_up, width),
        out_shape=(jax.ShapeDtypeStruct((tiles, ROWS, model), f32), jax.ShapeDtypeStruct((ROWS, hidden), f32)),
        in_specs=[pl.BlockSpec(memory_space=pl.ANY)] * 2,
        out_specs=(pl.BlockSpec(memory_space=pltpu.VMEM), pl.BlockSpec(memory_space=pltpu.VMEM)),
        scratch_shapes=[
            pltpu.VMEM((3, 64, 2) + block, f32),
            pltpu.VMEM((count, 64) + block, f32),
            pltpu.VMEM((5, 64) + block, f32),
            pltpu.VMEM((count, 8) + block, f32),
            pltpu.VMEM((count, 8) + block, f32),
            pltpu.VMEM((count, 16) + block, f32),
            pltpu.VMEM((count, 16) + block, f32),
            pltpu.VMEM((3, 16) + block, f32),
            pltpu.VMEM((count, 3, 4) + block, f32),
            pltpu.VMEM((3, 4) + block, f32),
            pltpu.VMEM((count, 3) + block, f32),
            pltpu.SemaphoreType.DMA((3,)),
            pltpu.SemaphoreType.DMA((count,)),
            pltpu.SemaphoreType.DMA((count,)),
            pltpu.SemaphoreType.DMA((count, 6)),
            pltpu.SemaphoreType.DMA((count, 6)),
            pltpu.SemaphoreType.DMA((count, 3)),
            pltpu.SemaphoreType.DMA((count, 3)),
            pltpu.SemaphoreType.DMA((count, 3)),
            pltpu.SemaphoreType.DMA((count, 3)),
        ],
        compiler_params=pltpu.CompilerParams(collective_id=1, has_side_effects=True, vmem_limit_bytes=VMEM_BYTES),
    )(grad_down.reshape(64, 2, tiles, ROWS, model), grad_up.reshape(64, 2, ROWS, hidden))
    return out_down.reshape(hidden // 128, model), out_up


def solution(mesh):
    group_size = mesh.shape['data']

    def local_step(tok_rows, w_up, w_down, heads, label_rows):
        total_rows = tok_rows.shape[0] * group_size
        num_classes = heads.shape[2]
        pre_act = jnp.dot(tok_rows, w_up, preferred_element_type=jnp.float32).astype(jnp.bfloat16)
        hidden = jax.nn.gelu(pre_act.astype(jnp.float32)).astype(jnp.bfloat16)
        trunk_out = tok_rows.astype(jnp.float32) + jnp.dot(hidden, w_down, preferred_element_type=jnp.float32)
        logits = jnp.einsum('bd,tdc->tbc', trunk_out.astype(jnp.bfloat16), heads, preferred_element_type=jnp.float32)
        onehot = (label_rows[:, :, None] == jnp.arange(num_classes)[None, None, :]).astype(jnp.float32)
        task_resid = (jax.nn.softmax(logits, axis=-1) - onehot) / total_rows
        heads_f32 = heads.astype(jnp.float32)
        head_gram = jnp.einsum('tdc,sde->tcse', heads_f32, heads_f32, precision=EXACT_PREC)
        res_outer = jnp.einsum('tbc,sbe->tcse', task_resid, task_resid, precision=EXACT_PREC)
        part_gram = jnp.sum(res_outer * head_gram, axis=(1, 3))
        mix_wts = solve_weights(part_gram)
        d_out = jnp.einsum('tbc,tdc->bd', task_resid * mix_wts[:, None, None], heads_f32, precision=EXACT_PREC).astype(jnp.bfloat16)
        grad_down = lax.dot_general(hidden, d_out, (((0,), (0,)), ((), ())), preferred_element_type=jnp.float32)
        d_hidden = lax.dot_general(d_out, w_down, (((1,), (1,)), ((), ())), preferred_element_type=jnp.float32)
        gelu_vjp = jax.vjp(jax.nn.gelu, pre_act.astype(jnp.float32))[1]
        d_pre = gelu_vjp(d_hidden)[0].astype(jnp.bfloat16)
        tok_cols = lax.optimization_barrier(tok_rows.T)
        grad_up = jnp.dot(tok_cols, d_pre, preferred_element_type=jnp.float32)
        down_shard, up_shard = scatter_grads(grad_down, grad_up, 512)
        return mix_wts, up_shard, down_shard

    return jax.shard_map(local_step, mesh=mesh, in_specs=(P('data', None), P(), P(), P(), P(None, 'data')), out_specs=(P(), P('data', None), P('data', None)), check_vma=False)
```

time: 1600 us -> 271 us (0.17)
  waiting for transfers between devices: 1310 us -> 0 us
  Pallas kernels: 0 us -> 109 us
  blocking collectives: 68.5 us -> 0 us
  other arithmetic: 28.4 us -> 1.91 us
    reduce_scatter x1 -> x0, waiting for transfers between devices: 669 us -> none  [local_step(): lax.psum_scatter(grad_down, 'data', scatter_dimension=0, tiled=True)]
    unnamed x3 -> x0, waiting for transfers between devices: 640 us -> none
    pallas_call x0 -> x2, Pallas kernels: none -> 109 us  [the longest x1 88.2 us: scatter_grads(): pl.pallas_call(functools.partial(scatter_kernel, n_down, n_up, width), ou...]
    psum x1 -> x0, blocking collectives: 68.5 us -> none  [local_step(): full_gram = lax.psum(part_gram, 'data')]
  transfers between devices with their start and end apart: 2 -> 0, of which waited for: 2 -> 0; matrix products, arithmetic and copies ran while one was open for 2% -> 0% of each run, Pallas kernels for 0% -> 0%
where the time goes in v1:
time: 271 us
  matrix products  156 us (58%)
  Pallas kernels  109 us (40%)
  local copies, waits for them, and re-layouts  3.26 us (1%)
    pallas_call x1, Pallas kernels, scatter_grads(): pl.pallas_call(functools.partial(scatter_kernel, n_down, n_up, width), ou...  88.2 us
    dot_general x1, matrix products, local_step(): lax.dot_general(d_out, w_down, (((1,), (1,)), ((), ())), preferred_elemen...  44.9 us
    dot_general x1, matrix products, local_step(): lax.dot_general(hidden, d_out, (((0,), (0,)), ((), ())), preferred_elemen...  30.1 us
    dot_general x1, matrix products, local_step(): jnp.einsum('bd,tdc->tbc', trunk_out.astype(jnp.bfloat16), heads, preferre...  28.5 us
    dot_general x1, matrix products, local_step(): jnp.dot(tok_rows, w_up, preferred_element_type=jnp.float32)  24.2 us
    dot_general x1, matrix products, local_step(): grad_up = jnp.dot(tok_cols, d_pre, preferred_element_type=jnp.float32)  23.3 us
    pallas_call x1, Pallas kernels, solve_weights(): pl.pallas_call(gram_kernel, out_shape=jax.ShapeDtypeStruct((8, 128), jnp....  20.7 us

profile of v1, /device:TPU:0, one launch (start us, length us, event | category | flops | bytes accessed | tf_op | source)
XLA Modules:
  0.0 271.1 jit_solution(17177813370305253851)
XLA Ops:
  0.6 0.0 copy-start.2
  0.6 24.2 %convolution_convert_fusion = bf16[2048,4096]{1,0:T(8,128)(2,1)} fusion(bf16[2048,1024]{1,0:T(8,128)(2,1)} %param.5, bf16[1024,4096]{1,0:T(8,128)(2,1)} %param.6), kind=kOutput, calls=%fused_computation.16 | convolution fusion | flops 17188257792 | bytes 29360128 | tf_op jit(solution)/shard_map/dot_general | solution.py:322
  24.8 0.0 copy-done.2
  24.8 0.0 copy-start
  24.8 28.5 %fusion.44 = (f32[4,2048]{1,0:T(4,128)S(1)}, f32[4,2048,3]{1,0,2:T(4,128)S(1)}) fusion(bf16[4,1024,3]{1,0,2:T(4,128)(2,1)S(1)} %copy-done.2, bf16[4096,1024]{1,0:T(8,128)(2,1)} %param.7, bf16[2048,4096]{1,0:T(8,128)(2,1)} %convolution_convert_fusion, bf16[2048,1024]{1,0:T(8,128)(2,1)} %param.5), kind=kOutput, calls=%fused_computation.51 | convolution fusion | flops 17320394752 | bytes 29515776 | tf_op jit(solution)/shard_map/bd,tdc->tbc/dot_general | solution.py:325
  53.3 0.1 fusion.25
  53.4 0.0 copy-done
  53.4 0.1 divide_subtract_fusion
  53.4 1.3 fusion.20
  54.7 0.2 fusion.19
  55.0 0.1 copy.9
  55.1 0.6 select_maximum_fusion.gram_ref
  55.7 20.7 %shard_map.76 = f32[8,128]{1,0:T(8,128)} custom-call(f32[2,8,128]{2,1,0:T(8,128)} %select_maximum_fusion.gram_ref), custom_call_target="tpu_custom_call" | custom-call | tf_op jit(solution)/shard_map/pallas_call | solution.py:87
  76.4 1.2 broadcast_multiply_fusion
  77.6 0.0 slice-start
  77.6 3.9 %bitcast_convert_fusion = bf16[2048,1024]{1,0:T(8,128)(2,1)S(1)} fusion(bf16[4,1024,3]{1,0,2:T(4,128)(2,1)S(1)} %copy-done.2, f32[4,2048,3]{1,0,2:T(4,128)S(1)} %divide_subtract_fusion, f32[4]{0:T(128)S(1)} %get-tuple-element.7), kind=kOutput, calls=%fused_computation.18 | convolution fusion | flops 304111616 | bytes 4317200 | tf_op jit(solution)/shard_map/tbc,tdc->bd/dot_general | solution.py:333
  81.5 0.0 copy-start.3
  81.5 0.0 slice-start.1
  81.5 30.1 %fusion.37 = f32[4096,1024]{1,0:T(8,128)} fusion(bf16[2048,1024]{1,0:T(8,128)(2,1)S(1)} %bitcast_convert_fusion, bf16[2048,4096]{1,0:T(8,128)(2,1)} %convolution_convert_fusion), kind=kOutput, calls=%fused_computation.50 | convolution fusion | flops 17263755264 | bytes 37748736 | tf_op jit(solution)/shard_map/dot_general | solution.py:334
  111.6 0.0 copy-done.3
  111.6 0.0 slice-done
  111.6 0.0 slice-done.1
  111.6 0.0 copy-start.1
  111.7 44.9 %fusion.65 = bf16[2048,4096]{1,0:T(8,128)(2,1)} fusion(bf16[2048,4096]{1,0:T(8,128)(2,1)} %convolution_convert_fusion, bf16[2048,1024]{1,0:T(8,128)(2,1)} %copy-done.3, bf16[4096,1024]{1,0:T(8,128)(2,1)S(1)} %bitcast.61), kind=kOutput, calls=%fused_computation.8.clone.clone.1 | convolution fusion | flops 17356029952 | bytes 46137344 | tf_op jit(solution)/shard_map/dot_general | solution.py:335
  156.5 0.0 copy-done.1
  156.5 23.3 %fusion.10 = f32[4096,1024]{0,1:T(8,128)} fusion(bf16[1024,2048]{0,1:T(8,128)(2,1)S(1)} %bitcast.62, bf16[2048,4096]{1,0:T(8,128)(2,1)} %fusion.65), kind=kOutput, calls=%fused_computation.15 | convolution fusion | flops 17179869184 | bytes 37748736 | tf_op jit(solution)/shard_map/dot_general | solution.py:339
  179.8 88.2 %shard_map.77 = (f32[4,8,1024]{2,1,0:T(8,128)}, f32[8,4096]{1,0:T(8,128)}) custom-call(f32[64,2,4,8,1024]{4,3,2,1,0:T(8,128)} %bitcast.54, f32[64,2,8,4096]{3,2,1,0:T(8,128)} %bitcast.55), custom_call_target="tpu_custom_call" | custom-call | tf_op jit(solution)/shard_map/pallas_call | solution.py:284
  268.0 1.6 copy.14
  269.6 1.6 copy.15
  (1 shorter events, 0.0 us)
Async XLA Ops:
  0.6 24.2 %copy-start.2 = (bf16[4,1024,3]{1,0,2:T(4,128)(2,1)S(1)}, bf16[4,1024,3]{1,0,2:T(4,128)(2,1)}, u32[]{:S(2)}) copy-start(bf16[4,1024,3]{1,0,2:T(4,128)(2,1)} %param.8) | copy-start | bytes 73732
  24.8 28.5 %copy-start = (s32[4,2048]{1,0:T(4,128)S(1)}, s32[4,2048]{1,0:T(4,128)}, u32[]{:S(2)}) copy-start(s32[4,2048]{1,0:T(4,128)} %param.9) | copy-start | bytes 98308
  77.6 34.0 %slice-start = ((s8[8388608]{0:T(1024)(128)(4,1)}), s8[4194304]{0:T(1024)(128)(4,1)S(1)}, s32[]{:S(2)}) async-start(s8[8388608]{0:T(1024)(128)(4,1)} %bitcast.60), calls=%async_computation | async-start | bytes 8388608
  81.5 30.1 %copy-start.3 = (bf16[2048,1024]{1,0:T(8,128)(2,1)}, bf16[2048,1024]{1,0:T(8,128)(2,1)S(1)}, u32[]{:S(2)}) copy-start(bf16[2048,1024]{1,0:T(8,128)(2,1)S(1)} %bitcast_convert_fusion) | copy-start | bytes 12582916
  81.5 30.1 %slice-start.1 = ((s8[8388608]{0:T(1024)(128)(4,1)}), s8[4194304]{0:T(1024)(128)(4,1)S(1)}, s32[]{:S(2)}) async-start(s8[8388608]{0:T(1024)(128)(4,1)} %bitcast.60), calls=%async_computation.1 | async-start | bytes 8388608
  111.6 44.9 %copy-start.1 = (bf16[2048,1024]{1,0:T(8,128)(2,1)S(1)}, bf16[2048,1024]{1,0:T(8,128)(2,1)}, u32[]{:S(2)}) copy-start(bf16[2048,1024]{1,0:T(8,128)(2,1)} %param.5) | copy-start | bytes 12582916

commit v2 on v1

v2 whole, which is shorter than its diff:
```python
import functools

import jax
import jax.numpy as jnp
from jax import lax
from jax.experimental import pallas as pl
from jax.experimental.pallas import tpu as pltpu
from jax.sharding import PartitionSpec as P

SOLVER_STEPS = 20
EXACT_PREC = lax.Precision.HIGHEST
MESH = pl.DeviceIdType.MESH
VMEM_BYTES = 67_043_328
ROWS = 8


def coords(me):
    return me % 2, (me // 2) % 4, (me // 8) % 4, me // 32


def axis_of(k, x, y, z):
    wz = (k - 1) * (k - 2) // 2
    wy = k * (2 - k)
    wx = k * (k - 1) // 2
    return z * wz + y * wy + x * wx, 32 * wz + 8 * wy + 2 * wx


def enter(peers):
    barrier = pltpu.get_barrier_semaphore()
    for peer in peers:
        pl.semaphore_signal(barrier, inc=1, device_id=(peer,), device_id_type=MESH)
    pl.semaphore_wait(barrier, len(peers))


def gram_kernel(gram_ref, tok_ref, wts_ref, cols_ref, stage0, stage1, stage2, tot0, tot1, send_sem, recv_sem):
    me = lax.axis_index('data')
    c, x, y, z = coords(me)
    low = me % 8
    group0 = [me - low + (low + d) % 8 for d in range(1, 8)]
    group1 = [me + ((y + d) % 4 - y) * 8 for d in range(1, 4)]
    group2 = [me + ((z + d) % 4 - z) * 32 for d in range(1, 4)]
    enter(group0 + group1 + group2)

    def exchange(src, slots, slot, group, first, beside=None):
        copies = []
        for n, peer in enumerate(group):
            copy = pltpu.make_async_remote_copy(
                src_ref=src,
                dst_ref=slots.at[slot],
                send_sem=send_sem.at[first + n],
                recv_sem=recv_sem.at[first + n],
                device_id=(peer,),
                device_id_type=MESH,
            )
            copy.start()
            copies.append(copy)
        slots[slot] = src[...]
        if beside is not None:
            beside()
        for copy in copies:
            copy.wait()

    def transpose():
        cols_ref[...] = tok_ref[...].T

    exchange(gram_ref, stage0, low, group0, 0, transpose)
    tot0[...] = sum(stage0[n] for n in range(1, 8)) + stage0[0]
    exchange(tot0, stage1, y, group1, 7)
    tot1[...] = (stage1[0] + stage1[1]) + (stage1[2] + stage1[3])
    exchange(tot1, stage2, z, group2, 10)
    full = (stage2[0] + stage2[1]) + (stage2[2] + stage2[3])
    gram, gram_t = full[0], full[1]
    row = lax.broadcasted_iota(jnp.int32, gram.shape, 0)
    lane = lax.broadcasted_iota(jnp.int32, gram.shape, 1)
    trace = jnp.sum(jnp.where(row == lane, gram, 0.0), axis=(0, 1), keepdims=True)
    scale = jnp.broadcast_to(trace / 4, gram.shape)
    by_lane = jnp.where(lane < 4, 0.25, 0.0)
    by_row = jnp.where(row < 4, 0.25, 0.0)
    for _ in range(SOLVER_STEPS):
        down_row = jnp.sum(gram * by_lane, axis=1, keepdims=True)
        down_lane = jnp.sum(gram_t * by_row, axis=0, keepdims=True)
        by_row = by_row * jnp.exp(-down_row / scale)
        by_lane = by_lane * jnp.exp(-down_lane / scale)
        by_row = by_row / jnp.sum(by_row, axis=0, keepdims=True)
        by_lane = by_lane / jnp.sum(by_lane, axis=1, keepdims=True)
    wts_ref[...] = by_lane


def solve_weights(part_gram, tok_rows):
    pads = ((0, 0), (0, 4), (0, 124))
    both = jnp.pad(jnp.stack([part_gram, part_gram.T]), pads)
    vmem = pl.BlockSpec(memory_space=pltpu.VMEM)
    wts, tok_cols = pl.pallas_call(
        gram_kernel,
        out_shape=(jax.ShapeDtypeStruct((8, 128), jnp.float32), jax.ShapeDtypeStruct(tok_rows.shape[::-1], tok_rows.dtype)),
        in_specs=[vmem, vmem],
        out_specs=(vmem, vmem),
        scratch_shapes=[
            pltpu.VMEM((8, 2, 8, 128), jnp.float32),
            pltpu.VMEM((4, 2, 8, 128), jnp.float32),
            pltpu.VMEM((4, 2, 8, 128), jnp.float32),
            pltpu.VMEM((2, 8, 128), jnp.float32),
            pltpu.VMEM((2, 8, 128), jnp.float32),
            pltpu.SemaphoreType.DMA((13,)),
            pltpu.SemaphoreType.DMA((13,)),
        ],
        compiler_params=pltpu.CompilerParams(collective_id=0, has_side_effects=True),
    )(both, tok_rows)
    return wts[0, :4], tok_cols


TOK = 512
WIDTH = 512
GELU_C = 0.7978845608028654
GELU_K = 0.044715


def backward_kernel(n_up, n_down, pre_ref, dz_ref, wd_ref, xt_ref, out_up, out_down,
                    xt, dz, p_t, pre, wd, d_pre, dh_a, dh_b, p_buf,
                    src, pair_in, work, opp_r, opp_l, from_l, from_r, mid, mid_in, low, low_in,
                    xt_sem, dz_sem, pre_sem, wd_sem, pair_s, pair_r, s1, r1, s2, r2, s3, r3):
    count = n_up + n_down
    me = lax.axis_index('data')
    c, x, y, z = coords(me)
    partner = me + 1 - 2 * c
    everyone = [partner]
    for k in range(3):
        pos, stride = axis_of(k, x, y, z)
        everyone += [me + ((pos + d) % 4 - pos) * stride for d in range(1, 4)]

    tiles = dz.shape[0] // TOK
    n_tiles = n_up * tiles

    def load_pre(g):
        rows = pl.ds(pl.multiple_of((g % tiles) * TOK, TOK), TOK)
        cols = pl.ds(pl.multiple_of((g // tiles) * WIDTH, WIDTH), WIDTH)
        return pltpu.make_async_copy(pre_ref.at[rows, cols], pre.at[g % 3], pre_sem.at[g % 3])

    def load_wd(j):
        rows = pl.ds(pl.multiple_of(j * WIDTH, WIDTH), WIDTH)
        return pltpu.make_async_copy(wd_ref.at[rows], wd.at[j % 2], wd_sem.at[j % 2])

    load_dz = pltpu.make_async_copy(dz_ref, dz, dz_sem)
    load_xt = pltpu.make_async_copy(xt_ref, xt, xt_sem)
    load_wd(0).start()
    load_dz.start()
    load_pre(0).start()
    load_pre(1).start()
    load_wd(1).start()
    load_xt.start()
    enter(everyone)

    def axes(u):
        return [axis_of((u + n) % 3, x, y, z) for n in range(3)]

    def remote(a, b, s, r, peer):
        return pltpu.make_async_remote_copy(
            src_ref=a, dst_ref=b, send_sem=s, recv_sem=r, device_id=(peer,), device_id_type=MESH)

    def pair_copy(u):
        return remote(src.at[u % 2, :, 1 - c], pair_in.at[u % 4], pair_s.at[u % 4], pair_r.at[u % 4], partner)

    def first_copies(u):
        pos, stride = axes(u)[0]
        right = me + ((pos + 1) % 4 - pos) * stride
        left = me + ((pos + 3) % 4 - pos) * stride
        at_r, at_l, at_o = 16 * ((pos + 1) % 4), 16 * ((pos + 3) % 4), 16 * ((pos + 2) % 4)
        buf = work.at[u % 4]
        ends = [
            (at_o, opp_r.at[u], right),
            (at_o + 8, opp_l.at[u], left),
            (at_r + 8, from_l.at[u, pl.ds(8, 8)], right),
            (at_l, from_r.at[u, pl.ds(0, 8)], left),
            (at_r, from_l.at[u, pl.ds(0, 8)], right),
            (at_l + 8, from_r.at[u, pl.ds(8, 8)], left),
        ]
        return [remote(buf.at[pl.ds(at, 8)], dst, s1.at[u, n], r1.at[u, n], peer) for n, (at, dst, peer) in enumerate(ends)]

    def second_copies(u):
        pos, stride = axes(u)[1]
        return [remote(mid.at[u % 3, pl.ds(4 * ((pos + d) % 4), 4)], mid_in.at[u, d - 1], s2.at[u, d - 1], r2.at[u, d - 1],
                       me + ((pos + d) % 4 - pos) * stride) for d in range(1, 4)]

    def third_copies(u):
        pos, stride = axes(u)[2]
        return [remote(low.at[u % 3, (pos + d) % 4], low_in.at[u, d - 1], s3.at[u, d - 1], r3.at[u, d - 1],
                       me + ((pos + d) % 4 - pos) * stride) for d in range(1, 4)]

    def within(u):
        return jnp.logical_and(u >= 0, u < count)

    def dh_dot(g, out):
        rows = pl.ds(pl.multiple_of((g % tiles) * TOK, TOK), TOK)
        out[...] = lax.dot_general(dz[rows], wd[(g // tiles) % 2], (((1,), (1,)), ((), ())), preferred_element_type=jnp.float32)

    def act_tile(g, dh):
        slot = g % 3
        at = pl.multiple_of((g % tiles) * TOK, TOK)
        for r in range(0, TOK, 32):
            v = pre[slot, r:r + 32].astype(jnp.float32)
            sq = v * v
            th = jnp.tanh(v * (GELU_C + (GELU_C * GELU_K) * sq))
            cdf = 0.5 + 0.5 * th
            p_buf[r:r + 32] = (v * cdf).astype(jnp.bfloat16)
            slope = cdf + (0.5 * v) * (1.0 - th * th) * (GELU_C + (3 * GELU_C * GELU_K) * sq)
            d_pre[pl.ds(at + r, 32)] = (dh[r:r + 32] * slope).astype(jnp.bfloat16)
        flipped = p_buf[...].T
        p_t[pl.ds(pl.multiple_of((g // tiles) * (WIDTH // 32), WIDTH // 32), WIDTH // 32), :, :, pl.ds(at, TOK)] = flipped.reshape(WIDTH // 32, 2, 16, TOK)

    def produce_up(t):
        @pl.when(t == 0)
        def _():
            load_wd(0).wait()
            load_dz.wait()
            dh_dot(0, dh_a)

        @pl.when(t + 1 < n_up)
        def _():
            load_wd(t + 1).wait()

        def step(i, _):
            for half, (now, then) in enumerate(((dh_a, dh_b), (dh_b, dh_a))):
                g = t * tiles + 2 * i + half

                @pl.when(g + 2 < n_tiles)
                def _():
                    load_pre(g + 2).start()

                load_pre(g).wait()
                dh_dot(g + 1, then)
                act_tile(g, now)
            return 0

        lax.fori_loop(0, tiles // 2, step, 0)

        @pl.when(t + 2 < n_up)
        def _():
            load_wd(t + 2).start()

        @pl.when(t == 0)
        def _():
            load_xt.wait()

        prod = jnp.dot(xt[...], d_pre[...], preferred_element_type=jnp.float32)
        src[t % 2] = prod.reshape(64, 2, ROWS, WIDTH)

    def produce_down(t):
        u = t - n_up
        half = u % 2
        cols = pl.ds(pl.multiple_of((u // 2) * 256, 256), 256)
        for m in range(2):
            rows = p_t[pl.ds(64 * m, 64), half].reshape(1024, p_t.shape[3])
            prod = jnp.dot(rows, dz[:, cols], preferred_element_type=jnp.float32)
            prod = prod.reshape(32, 2, 2, ROWS, 256)
            src[t % 2, pl.ds(32 * m, 32), :, :, 0:256] = prod[:, :, 0]
            src[t % 2, pl.ds(32 * m, 32), :, :, 256:512] = prod[:, :, 1]

    def body(t, _):
        @pl.when(t < n_up)
        def _():
            produce_up(t)

        @pl.when(jnp.logical_and(t >= n_up, t < count))
        def _():
            produce_down(t)

        @pl.when(t < count)
        def _():
            pair_copy(t).start()

        uc = t - 3

        @pl.when(within(uc))
        def _():
            copies = first_copies(uc)
            (pos, _), _, _ = axes(uc)
            at_r, at_l = 16 * ((pos + 1) % 4), 16 * ((pos + 3) % 4)
            copies[0].wait_recv()
            work[uc % 4, pl.ds(at_r, 8)] += opp_r[uc]
            copies[4].start()
            copies[1].wait_recv()
            work[uc % 4, pl.ds(at_l + 8, 8)] += opp_l[uc]
            copies[5].start()

        ud = t - 5

        @pl.when(within(ud))
        def _():
            copies = first_copies(ud)
            for copy in copies[2:]:
                copy.wait_recv()
            (pos, _), _, _ = axes(ud)
            for n in range(0, 16, 4):
                mid[ud % 3, pl.ds(n, 4)] = (work[ud % 4, pl.ds(16 * pos + n, 4)] + from_l[ud, pl.ds(n, 4)]) + from_r[ud, pl.ds(n, 4)]
            for copy in second_copies(ud):
                copy.start()
            for copy in copies:
                copy.wait_send()

        ub = t - 1

        @pl.when(within(ub))
        def _():
            copy = pair_copy(ub)
            copy.wait_recv()
            (_, st1), (_, st2), (_, st3) = axes(ub)

            def add(b, _):
                at = (b // 4) * (st1 // 2) + (b % 4) * (st2 // 2)
                for n in range(4):
                    here = at + n * (st3 // 2)
                    work[ub % 4, 4 * b + n] = src[ub % 2, here, c] + pair_in[ub % 4, here]
                return 0

            lax.fori_loop(0, 16, add, 0)
            copy.wait_send()
            for copy in first_copies(ub)[:4]:
                copy.start()

        ue = t - 7

        @pl.when(within(ue))
        def _():
            copies = second_copies(ue)
            for copy in copies:
                copy.wait_recv()
            _, (pos, _), _ = axes(ue)
            low[ue % 3] = (mid[ue % 3, pl.ds(4 * pos, 4)] + mid_in[ue, 0]) + (mid_in[ue, 1] + mid_in[ue, 2])
            for copy in third_copies(ue):
                copy.start()
            for copy in copies:
                copy.wait_send()

        uf = t - 9

        @pl.when(within(uf))
        def _():
            copies = third_copies(uf)
            for copy in copies:
                copy.wait_recv()
            _, _, (pos, _) = axes(uf)
            total = (low[uf % 3, pos] + low_in[uf, 0]) + (low_in[uf, 1] + low_in[uf, 2])

            @pl.when(uf < n_up)
            def _():
                out_up[:, pl.ds(pl.multiple_of(uf * WIDTH, WIDTH), WIDTH)] = total

            @pl.when(uf >= n_up)
            def _():
                tile = uf - n_up
                cols = pl.ds(pl.multiple_of((tile // 2) * 256, 256), 256)
                out_down[2 * (tile % 2), :, cols] = total[:, 0:256]
                out_down[2 * (tile % 2) + 1, :, cols] = total[:, 256:512]

            for copy in copies:
                copy.wait_send()

        return 0

    lax.fori_loop(0, count + 9, body, 0)


def backward(pre_act, d_out, w_down, tok_cols):
    tokens, hidden = pre_act.shape
    model = d_out.shape[1]
    n_up, n_down = hidden // WIDTH, 2 * (model // 256)
    count = n_up + n_down
    f32, bf16 = jnp.float32, jnp.bfloat16
    block = (ROWS, WIDTH)
    dma = pltpu.SemaphoreType.DMA
    out_up, out_down = pl.pallas_call(
        functools.partial(backward_kernel, n_up, n_down),
        out_shape=(jax.ShapeDtypeStruct((ROWS, hidden), f32), jax.ShapeDtypeStruct((4, ROWS, model), f32)),
        in_specs=[pl.BlockSpec(memory_space=pl.ANY)] * 4,
        out_specs=(pl.BlockSpec(memory_space=pltpu.VMEM), pl.BlockSpec(memory_space=pltpu.VMEM)),
        scratch_shapes=[
            pltpu.VMEM((model, tokens), bf16),
            pltpu.VMEM((tokens, model), bf16),
            pltpu.VMEM((hidden // 32, 2, 16, tokens), bf16),
            pltpu.VMEM((3, TOK, WIDTH), bf16),
            pltpu.VMEM((2, WIDTH, model), bf16),
            pltpu.VMEM((tokens, WIDTH), bf16),
            pltpu.VMEM((TOK, WIDTH), f32),
            pltpu.VMEM((TOK, WIDTH), f32),
            pltpu.VMEM((TOK, WIDTH), bf16),
            pltpu.VMEM((2, 64, 2) + block, f32),
            pltpu.VMEM((4, 64) + block, f32),
            pltpu.VMEM((4, 64) + block, f32),
            pltpu.VMEM((count, 8) + block, f32),
            pltpu.VMEM((count, 8) + block, f32),
            pltpu.VMEM((count, 16) + block, f32),
            pltpu.VMEM((count, 16) + block, f32),
            pltpu.VMEM((3, 16) + block, f32),
            pltpu.VMEM((count, 3, 4) + block, f32),
            pltpu.VMEM((3, 4) + block, f32),
            pltpu.VMEM((count, 3) + block, f32),
            dma, dma, dma((3,)), dma((2,)), dma((4,)), dma((4,)),
            dma((count, 6)), dma((count, 6)), dma((count, 3)), dma((count, 3)), dma((count, 3)), dma((count, 3)),
        ],
        compiler_params=pltpu.CompilerParams(collective_id=1, has_side_effects=True, vmem_limit_bytes=VMEM_BYTES),
    )(pre_act, d_out, w_down, tok_cols)
    return out_up, out_down.reshape(hidden // 128, model)


def solution(mesh):
    group_size = mesh.shape['data']

    def local_step(tok_rows, w_up, w_down, heads, label_rows):
        total_rows = tok_rows.shape[0] * group_size
        num_classes = heads.shape[2]
        pre_act = jnp.dot(tok_rows, w_up, preferred_element_type=jnp.float32).astype(jnp.bfloat16)
        hidden = jax.nn.gelu(pre_act.astype(jnp.float32)).astype(jnp.bfloat16)
        trunk_out = tok_rows.astype(jnp.float32) + jnp.dot(hidden, w_down, preferred_element_type=jnp.float32)
        logits = jnp.einsum('bd,tdc->tbc', trunk_out.astype(jnp.bfloat16), heads, preferred_element_type=jnp.float32)
        onehot = (label_rows[:, :, None] == jnp.arange(num_classes)[None, None, :]).astype(jnp.float32)
        task_resid = (jax.nn.softmax(logits, axis=-1) - onehot) / total_rows
        heads_f32 = heads.astype(jnp.float32)
        head_gram = jnp.einsum('tdc,sde->tcse', heads_f32, heads_f32, precision=EXACT_PREC)
        res_outer = jnp.einsum('tbc,sbe->tcse', task_resid, task_resid, precision=EXACT_PREC)
        part_gram = jnp.sum(res_outer * head_gram, axis=(1, 3))
        mix_wts, tok_cols = solve_weights(part_gram, tok_rows)
        d_out = jnp.einsum('tbc,tdc->bd', task_resid * mix_wts[:, None, None], heads_f32, precision=EXACT_PREC).astype(jnp.bfloat16)
        up_shard, down_shard = backward(pre_act, d_out, w_down, tok_cols)
        return mix_wts, up_shard, down_shard

    return jax.shard_map(local_step, mesh=mesh, in_specs=(P('data', None), P(), P(), P(), P(None, 'data')), out_specs=(P(), P('data', None), P('data', None)), check_vma=False)
```

time: 271 us -> 216 us (0.80)
  matrix products: 156 us -> 59.4 us
  Pallas kernels: 109 us -> 151 us
    dot_general x3 -> x0, matrix products: 98.2 us -> none  [the longest x1 44.9 us: local_step(): lax.dot_general(d_out, w_down, (((1,), (1,)), ((), ())), preferred_elemen...]
    pallas_call x2, Pallas kernels: 109 us -> 151 us  [the longest x1 129 us: backward(): pl.pallas_call(functools.partial(backward_kernel, n_up, n_down), out_shap...]
where the time goes in v2:
time: 216 us
  Pallas kernels  151 us (70%)
  matrix products  59.4 us (28%)
  local copies, waits for them, and re-layouts  3.24 us (2%)
    pallas_call x1, Pallas kernels, backward(): pl.pallas_call(functools.partial(backward_kernel, n_up, n_down), out_shap...  129 us
    dot_general x1, matrix products, local_step(): jnp.einsum('bd,tdc->tbc', trunk_out.astype(jnp.bfloat16), heads, preferre...  28.5 us
    dot_general x1, matrix products, local_step(): jnp.dot(tok_rows, w_up, preferred_element_type=jnp.float32)  24.2 us
    pallas_call x1, Pallas kernels, solve_weights(): pl.pallas_call(gram_kernel, out_shape=(jax.ShapeDtypeStruct((8, 128), jnp...  22.2 us
    dot_general x1, matrix products, local_step(): jnp.einsum('tbc,tdc->bd', task_resid * mix_wts[:, None, None], heads_f32,...  5.22 us

profile of v2, /device:TPU:0, one launch (start us, length us, event | category | flops | bytes accessed | tf_op | source)
XLA Modules:
  0.0 216.1 jit_solution(17837341274382118657)
XLA Ops:
  0.6 0.0 copy-start.1
  0.6 24.2 %convolution_convert_fusion.pre_ref = bf16[2048,4096]{1,0:T(8,128)(2,1)} fusion(bf16[2048,1024]{1,0:T(8,128)(2,1)} %tok_ref.1, bf16[1024,4096]{1,0:T(8,128)(2,1)} %param.6), kind=kOutput, calls=%fused_computation.11 | convolution fusion | flops 17188257792 | bytes 29360128 | tf_op jit(solution)/shard_map/dot_general | solution.py:411
  24.8 0.0 copy-done.1
  24.8 0.0 copy-start
  24.8 28.5 %fusion.39 = (f32[4,2048]{1,0:T(4,128)S(1)}, f32[4,2048,3]{1,0,2:T(4,128)S(1)}) fusion(bf16[4,1024,3]{1,0,2:T(4,128)(2,1)S(1)} %copy-done.1, bf16[4096,1024]{1,0:T(8,128)(2,1)} %wd_ref.1, bf16[2048,4096]{1,0:T(8,128)(2,1)} %convolution_convert_fusion.pre_ref, bf16[2048,1024]{1,0:T(8,128)(2,1)} %tok_ref.1), kind=kOutput, calls=%fused_computation.42 | convolution fusion | flops 17320394752 | bytes 29515776 | tf_op jit(solution)/shard_map/bd,tdc->tbc/dot_general | solution.py:414
  53.3 0.1 fusion.25
  53.4 0.0 copy-done
  53.4 0.1 divide_subtract_fusion
  53.4 1.3 fusion.20
  54.8 0.2 fusion.15
  55.0 0.1 copy.9
  55.1 0.6 select_maximum_fusion.gram_ref
  55.7 22.2 %shard_map.76 = (f32[8,128]{1,0:T(8,128)}, bf16[1024,2048]{1,0:T(8,128)(2,1)}) custom-call(f32[2,8,128]{2,1,0:T(8,128)} %select_maximum_fusion.gram_ref, bf16[2048,1024]{1,0:T(8,128)(2,1)} %tok_ref.1), custom_call_target="tpu_custom_call" | custom-call | tf_op jit(solution)/shard_map/pallas_call | solution.py:93
  77.9 1.2 broadcast_multiply_fusion
  79.1 5.2 %bitcast_convert_fusion.dz_ref = bf16[2048,1024]{1,0:T(8,128)(2,1)} fusion(bf16[4,1024,3]{1,0,2:T(4,128)(2,1)S(1)} %copy-done.1, f32[4,2048,3]{1,0,2:T(4,128)S(1)} %divide_subtract_fusion, f32[4]{0:T(128)S(1)} %get-tuple-element.11), kind=kOutput, calls=%fused_computation.12 | convolution fusion | flops 304111616 | bytes 4317200 | tf_op jit(solution)/shard_map/tbc,tdc->bd/dot_general | solution.py:422
  84.3 128.6 %shard_map.77 = (f32[8,4096]{1,0:T(8,128)}, f32[4,8,1024]{2,1,0:T(8,128)}) custom-call(bf16[2048,4096]{1,0:T(8,128)(2,1)} %convolution_convert_fusion.pre_ref, bf16[2048,1024]{1,0:T(8,128)(2,1)} %bitcast_convert_fusion.dz_ref, bf16[4096,1024]{1,0:T(8,128)(2,1)} %wd_ref.1, bf16[1024,2048]{1,0:T(8,128)(2,1)} %get-tuple-element.8.xt_ref), custom_call_target="tpu_custom_call" | custom-call | tf_op jit(solution)/shard_map/pallas_call | solution.py:371
  212.9 1.6 copy.14
  214.5 1.6 copy.15
Async XLA Ops:
  0.6 24.2 %copy-start.1 = (bf16[4,1024,3]{1,0,2:T(4,128)(2,1)S(1)}, bf16[4,1024,3]{1,0,2:T(4,128)(2,1)}, u32[]{:S(2)}) copy-start(bf16[4,1024,3]{1,0,2:T(4,128)(2,1)} %param.8) | copy-start | bytes 73732
  24.8 28.5 %copy-start = (s32[4,2048]{1,0:T(4,128)S(1)}, s32[4,2048]{1,0:T(4,128)}, u32[]{:S(2)}) copy-start(s32[4,2048]{1,0:T(4,128)} %param.9) | copy-start | bytes 98308
